TPU v7x, 128 devices: a whole 4x4x4 slice. The times are simulated.
128 devices in a mesh: chan: 8 (over x, core), tile: 16 (over z, y).
Axes of the slice: x: 4, y: 4, z: 4, core: 2. Of those that a mesh axis runs over, the one named last changes fastest.
Arguments:
- voltages: bfloat16 [8, 2, 2048, 2048], P(None, None, 'tile', 'chan'), may hold values from -16 to 16
- rfi_flags: int32 [8], P('chan'), may hold values 0 or 1
- beam_steer_index: int32 [8, 8], P('chan'), may hold values from 0 to 2047
- start_columns: int32 [8, 32], P('chan'), may hold values from 0 to 2047, as said below
Outputs:
- covariance: float32 [8, 2, 2048, 2048], P('chan', None, 'tile')
- weights: float32 [8, 8, 2, 2048], P('chan', None, None, 'tile')
Inputs may be any that keep to these rules, and one draw needn't show every extreme that they name: `start_columns`: the 32 antenna numbers of one channel are distinct.
All inputs are finite; a program needn't handle non-finite values. No bound on the sum of `rfi_flags` on one device may be relied on, other than what follows from the above.
Results may differ from a plain program's by a relative error of at most 0.0003.
Values may be sent and summed in bfloat16 or wider, within the bound.
No kernel may reach another device: no remote copies, remote signals or barrier semaphores. Data moves between devices by JAX's collectives and lax.ppermute only.
A program may use at most 128 MiB of HBM per device.

v0:
```python
import functools
import math
import jax
import jax.numpy as jnp
from jax import lax
from jax.sharding import Mesh
from jax.sharding import PartitionSpec as P

ARRAY_ELEMENTS = 2048
SNAPSHOT_COUNT = 2048
SUB_ITERS = 4
CG_ITERS = 12
TILE = ("tile_0", "tile_1")
diagonal_loading = 0.1
highest = lax.Precision.HIGHEST


def one_axis_at_a_time(shard, axes):
    return functools.reduce(lax.psum, axes, shard)


def from_everyone(shard, axis):
    devices = lax.axis_size(axis)
    return lax.all_to_all(
        jnp.broadcast_to(shard[None], (devices, *shard.shape)), axis, 0, 0, tiled=True
    )


def laid_out(pieces, dim):
    pieces = jnp.moveaxis(pieces, 0, dim)
    dims = pieces.shape
    return pieces.reshape(*dims[:dim], dims[dim] * dims[dim + 1], *dims[dim + 2 :])


def gathered_copies(shard, axis, dim):
    pieces = from_everyone(shard, axis)
    return laid_out(pieces, dim)


def steering_table(beam_entries):
    element_index = jnp.arange(ARRAY_ELEMENTS, dtype=jnp.int32)
    steer_phases = (beam_entries[..., None] * element_index % ARRAY_ELEMENTS).astype(
        jnp.float32
    ) * (2.0 * math.pi / ARRAY_ELEMENTS)
    return jnp.stack([jnp.cos(steer_phases), jnp.sin(steer_phases)], axis=-2)


def orthonormal(vectors):
    dims_in = vectors.shape
    flattened = vectors.reshape(dims_in[:-2] + (dims_in[-2] * dims_in[-1],))
    gram_matrix = jnp.einsum("...kx,...lx->...kl", flattened, flattened, precision=highest)
    factor = jnp.linalg.cholesky(gram_matrix)
    solved = lax.linalg.triangular_solve(factor, flattened, left_side=True, lower=True)
    return solved.reshape(dims_in)


def apply_rows(covariance, vectors):
    upper_half = vectors[..., 0, :]
    lower_half = vectors[..., 1, :]
    stacked = jnp.stack(
        [jnp.stack([upper_half, -lower_half], -2), jnp.stack([lower_half, upper_half], -2)], -3
    )
    return jnp.einsum("...bhpa,...pra->...bhr", stacked, covariance, precision=highest)


def project(vectors, subspace):
    coefficients = jnp.einsum("...bha,...kha->...bk", vectors, subspace, precision=highest)
    return vectors - jnp.einsum("...bk,...kha->...bha", coefficients, subspace, precision=highest)


def shards(voltages, rfi_flags, beam_steer_index, start_columns):
    turned = lax.all_to_all(voltages, "chan", split_axis=0, concat_axis=3, tiled=True)
    tile_total_count = lax.axis_size(TILE)
    block_row_set = ARRAY_ELEMENTS // tile_total_count
    first_row = lax.axis_index(TILE) * block_row_set
    gathered = lax.all_gather(turned, TILE, axis=2, tiled=True)
    own_rows = lax.dynamic_slice_in_dim(gathered, first_row, block_row_set, 3)
    swapped = jnp.stack([own_rows[:, 1], -own_rows[:, 0]], 1)
    real_part = jnp.einsum("cpsi,cpsj->cij", own_rows, gathered, preferred_element_type=jnp.float32)
    imag_part = jnp.einsum("cpsi,cpsj->cij", swapped, gathered, preferred_element_type=jnp.float32)
    summed = jnp.stack([real_part, imag_part], 1)
    covariance = summed * (1.0 / SNAPSHOT_COUNT)
    diagonal = lax.dynamic_slice_in_dim(covariance[:, 0], first_row, block_row_set, 2)
    covariance_trace = one_axis_at_a_time(
        jnp.sum(jnp.diagonal(diagonal, axis1=1, axis2=2), axis=1), TILE
    )
    loading_amount = diagonal_loading * covariance_trace / ARRAY_ELEMENTS
    picked = jnp.take_along_axis(covariance, start_columns[:, None, None, :], axis=3)
    col_real = jnp.swapaxes(picked[:, 0], 1, 2)
    col_imag = jnp.swapaxes(picked[:, 1], 1, 2)
    rows_now = jnp.concatenate(
        [jnp.stack([col_real, col_imag], 2), jnp.stack([-col_imag, col_real], 2)], 1
    )
    for sweep_index in range(SUB_ITERS):
        full_rows = gathered_copies(rows_now, TILE, 3)
        subspace = orthonormal(full_rows)
        if sweep_index + 1 < SUB_ITERS:
            rows_now = apply_rows(covariance, subspace)
    subspace = subspace * rfi_flags.astype(jnp.float32)[:, None, None, None]
    steering = steering_table(beam_steer_index)
    load_wide = loading_amount[:, None, None, None]
    load_narrow = loading_amount[:, None]

    def cg_sweep(counter, state_tuple):
        solved_weights, residual, direction, res_norm = state_tuple
        projected = project(direction, subspace)
        mapped = gathered_copies(apply_rows(covariance, projected), TILE, 3)
        combined = project(mapped, subspace) + load_wide * direction
        curvature = jnp.sum(projected * mapped, axis=(2, 3)) + load_narrow * jnp.sum(
            direction * direction, axis=(2, 3)
        )
        step_size = res_norm / curvature
        solved_weights = solved_weights + step_size[:, :, None, None] * direction
        residual = residual - step_size[:, :, None, None] * combined
        new_norm = jnp.sum(residual * residual, axis=(2, 3))
        direction = residual + (new_norm / res_norm)[:, :, None, None] * direction
        return (solved_weights, residual, direction, new_norm)

    start_state = (
        jnp.zeros_like(steering),
        steering,
        steering,
        jnp.sum(steering * steering, axis=(2, 3)),
    )
    solved_weights = lax.fori_loop(0, CG_ITERS, cg_sweep, start_state)[0]
    array_response = jnp.sum(steering * solved_weights, axis=(2, 3))
    weights = ARRAY_ELEMENTS * solved_weights / array_response[:, :, None, None]
    shard_local_rows = lax.dynamic_slice_in_dim(weights, first_row, block_row_set, 3)
    return (covariance, shard_local_rows)


def solution(mesh):
    split = Mesh(mesh.devices.reshape(mesh.shape["chan"], 4, 4), ("chan", "tile_0", "tile_1"))
    return jax.shard_map(
        shards,
        mesh=split,
        in_specs=(P(None, None, TILE, "chan"), P("chan"), P("chan", None), P("chan", None)),
        out_specs=(P("chan", None, TILE, None), P("chan", None, None, TILE)),
        check_vma=False,
    )
```

profile of v0, /device:TPU:0, one launch (start us, length us, event | category | flops | bytes accessed | tf_op | source)
XLA Modules:
  0.0 599.7 jit_solution(14355733121557029052)
XLA Ops:
  7.2 20.4 %all_to_all.45 = bf16[8,2,128,256]{3,2,1,0:T(8,128)(2,1)S(1)} all-to-all(bf16[8,2,128,256]{3,2,1,0:T(8,128)(2,1)} %param.9), channel_id=1, replica_groups=mesh['chan'=8,'tile_0'=4,'tile_1'=4] {'chan'}, dimensions={0} | all-to-all | bytes 2097152 | tf_op jit(solution)/shard_map/all_to_all | solution.py:72
  28.8 112.0 %all-gather.2.cloned.1.call-done = bf16[1,2,2048,2048]{3,2,1,0:T(8,128)(2,1)} async-done(((bf16[1,2,128,2048]{3,2,1,0:T(8,128)(2,1)}), bf16[1,2,2048,2048]{3,2,1,0:T(8,128)(2,1)}) %all-gather.2.cloned.1.call-update) | async-done | bytes 16777232 | tf_op jit(solution)/shard_map/all_gather | solution.py:76
  140.7 8.6 %fusion.26 = f32[128,2048,1]{1,0,2:T(8,128)S(1)} fusion(bf16[1,2,2048,2048]{3,2,1,0:T(8,128)(2,1)} %all-gather.2.cloned.1.call-done, s32[]{:T(128)S(6)} %select_n.91), kind=kOutput, calls=%fused_computation.39 | convolution fusion | flops 2147483648 | bytes 18874372 | tf_op jit(solution)/shard_map/cpsi,cpsj->cij/dot_general | solution.py:79
  162.4 22.2 %all_to_all.46 = f32[16,1,64,2,128]{4,2,3,1,0:T(8,128)S(1)} all-to-all(f32[16,1,64,2,128]{4,2,3,1,0:T(8,128)S(1)} %broadcast_in_dim.49), channel_id=1, replica_groups=mesh['chan'=8,'tile_0'=4,'tile_1'=4] {'tile_0','tile_1'}, dimensions={0} | all-to-all | bytes 2097152 | tf_op jit(solution)/shard_map/all_to_all | solution.py:24
  185.7 5.8 custom-call.15
  206.6 19.4 %all_to_all.47 = f32[16,1,64,2,128]{4,2,3,1,0:T(8,128)S(1)} all-to-all(f32[16,1,64,2,128]{4,2,3,1,0:T(8,128)S(1)} %broadcast_in_dim.74), channel_id=1, replica_groups=mesh['chan'=8,'tile_0'=4,'tile_1'=4] {'tile_0','tile_1'}, dimensions={0} | all-to-all | bytes 2097152 | tf_op jit(solution)/shard_map/all_to_all | solution.py:24
  227.1 5.8 custom-call.17
  254.3 14.5 %all-to-all-done.4 = f32[16,1,64,2,128]{4,2,3,1,0:T(8,128)S(1)} async-done(((f32[16,1,64,2,128]{4,2,3,1,0:T(8,128)}), f32[16,1,64,2,128]{4,2,3,1,0:T(8,128)S(1)}, u32[]{:S(2)}, u32[]{:S(2)}) %all-to-all-start.4) | async-done | bytes 1048608 | tf_op jit(solution)/shard_map/all_to_all | solution.py:24
  269.8 5.8 custom-call.19
  300.5 11.9 %psum.14 = f32[1]{0:T(128)} all-reduce(f32[1]{0:T(128)} %bitcast.91), channel_id=1, replica_groups=mesh['chan'=8,'tile_0'=4,'tile_1'=4] {'tile_0'}, use_global_device_ids=true, to_apply=%region_4.7 | all-reduce | flops 1 | bytes 8 | tf_op jit(solution)/shard_map/psum | solution.py:19
  313.3 10.8 %psum.15 = f32[1]{0:T(128)} all-reduce(f32[1]{0:T(128)} %psum.14), channel_id=1, replica_groups=mesh['chan'=8,'tile_0'=4,'tile_1'=4] {'tile_1'}, use_global_device_ids=true, to_apply=%region_5.8 | all-reduce | flops 1 | bytes 8 | tf_op jit(solution)/shard_map/psum | solution.py:19
  343.1 246.5 %while.17 = (s32[]{:T(128)}, f32[1,8,2,2048]{3,1,2,0:T(8,128)}, f32[1,8,2,2048]{3,1,2,0:T(8,128)}, f32[1,8,2,2048]{3,1,2,0:T(8,128)S(1)}, f32[1,8]{1,0:T(1,128)S...) while((s32[]{:T(128)}, f32[1,8,2,2048]{3,1,2,0:T(8,128)}, ...), condition=%wide.region_10.13_spmd.clone, body=%wide.region_6.12_spmd.clone.sunk | while | flops 202031136 | bytes 11035319 | solution.py:125
  350.8 7.8 %all-to-all-done = f32[16,1,8,2,128]{4,2,3,1,0:T(8,128)S(1)} async-done(((f32[16,1,8,2,128]{4,2,3,1,0:T(8,128)}), f32[16,1,8,2,128]{4,2,3,1,0:T(8,128)S(1)}, u32[]{:S(2)}, u32[]{:S(2)}) %all-to-all-start) | async-done | bytes 131104 | tf_op jit(solution)/shard_map/while/body/eval_jaxpr/all_to_all | solution.py:24
  371.3 7.8 %all-to-all-done = f32[16,1,8,2,128]{4,2,3,1,0:T(8,128)S(1)} async-done(((f32[16,1,8,2,128]{4,2,3,1,0:T(8,128)}), f32[16,1,8,2,128]{4,2,3,1,0:T(8,128)S(1)}, u32[]{:S(2)}, u32[]{:S(2)}) %all-to-all-start) | async-done | bytes 131104 | tf_op jit(solution)/shard_map/while/body/eval_jaxpr/all_to_all | solution.py:24
  391.9 7.8 %all-to-all-done = f32[16,1,8,2,128]{4,2,3,1,0:T(8,128)S(1)} async-done(((f32[16,1,8,2,128]{4,2,3,1,0:T(8,128)}), f32[16,1,8,2,128]{4,2,3,1,0:T(8,128)S(1)}, u32[]{:S(2)}, u32[]{:S(2)}) %all-to-all-start) | async-done | bytes 131104 | tf_op jit(solution)/shard_map/while/body/eval_jaxpr/all_to_all | solution.py:24
  412.4 7.8 %all-to-all-done = f32[16,1,8,2,128]{4,2,3,1,0:T(8,128)S(1)} async-done(((f32[16,1,8,2,128]{4,2,3,1,0:T(8,128)}), f32[16,1,8,2,128]{4,2,3,1,0:T(8,128)S(1)}, u32[]{:S(2)}, u32[]{:S(2)}) %all-to-all-start) | async-done | bytes 131104 | tf_op jit(solution)/shard_map/while/body/eval_jaxpr/all_to_all | solution.py:24
  432.9 7.8 %all-to-all-done = f32[16,1,8,2,128]{4,2,3,1,0:T(8,128)S(1)} async-done(((f32[16,1,8,2,128]{4,2,3,1,0:T(8,128)}), f32[16,1,8,2,128]{4,2,3,1,0:T(8,128)S(1)}, u32[]{:S(2)}, u32[]{:S(2)}) %all-to-all-start) | async-done | bytes 131104 | tf_op jit(solution)/shard_map/while/body/eval_jaxpr/all_to_all | solution.py:24
  453.5 7.8 %all-to-all-done = f32[16,1,8,2,128]{4,2,3,1,0:T(8,128)S(1)} async-done(((f32[16,1,8,2,128]{4,2,3,1,0:T(8,128)}), f32[16,1,8,2,128]{4,2,3,1,0:T(8,128)S(1)}, u32[]{:S(2)}, u32[]{:S(2)}) %all-to-all-start) | async-done | bytes 131104 | tf_op jit(solution)/shard_map/while/body/eval_jaxpr/all_to_all | solution.py:24
  474.0 7.8 %all-to-all-done = f32[16,1,8,2,128]{4,2,3,1,0:T(8,128)S(1)} async-done(((f32[16,1,8,2,128]{4,2,3,1,0:T(8,128)}), f32[16,1,8,2,128]{4,2,3,1,0:T(8,128)S(1)}, u32[]{:S(2)}, u32[]{:S(2)}) %all-to-all-start) | async-done | bytes 131104 | tf_op jit(solution)/shard_map/while/body/eval_jaxpr/all_to_all | solution.py:24
  494.6 7.8 %all-to-all-done = f32[16,1,8,2,128]{4,2,3,1,0:T(8,128)S(1)} async-done(((f32[16,1,8,2,128]{4,2,3,1,0:T(8,128)}), f32[16,1,8,2,128]{4,2,3,1,0:T(8,128)S(1)}, u32[]{:S(2)}, u32[]{:S(2)}) %all-to-all-start) | async-done | bytes 131104 | tf_op jit(solution)/shard_map/while/body/eval_jaxpr/all_to_all | solution.py:24
  515.1 7.8 %all-to-all-done = f32[16,1,8,2,128]{4,2,3,1,0:T(8,128)S(1)} async-done(((f32[16,1,8,2,128]{4,2,3,1,0:T(8,128)}), f32[16,1,8,2,128]{4,2,3,1,0:T(8,128)S(1)}, u32[]{:S(2)}, u32[]{:S(2)}) %all-to-all-start) | async-done | bytes 131104 | tf_op jit(solution)/shard_map/while/body/eval_jaxpr/all_to_all | solution.py:24
  535.6 7.8 %all-to-all-done = f32[16,1,8,2,128]{4,2,3,1,0:T(8,128)S(1)} async-done(((f32[16,1,8,2,128]{4,2,3,1,0:T(8,128)}), f32[16,1,8,2,128]{4,2,3,1,0:T(8,128)S(1)}, u32[]{:S(2)}, u32[]{:S(2)}) %all-to-all-start) | async-done | bytes 131104 | tf_op jit(solution)/shard_map/while/body/eval_jaxpr/all_to_all | solution.py:24
  556.2 7.8 %all-to-all-done = f32[16,1,8,2,128]{4,2,3,1,0:T(8,128)S(1)} async-done(((f32[16,1,8,2,128]{4,2,3,1,0:T(8,128)}), f32[16,1,8,2,128]{4,2,3,1,0:T(8,128)S(1)}, u32[]{:S(2)}, u32[]{:S(2)}) %all-to-all-start) | async-done | bytes 131104 | tf_op jit(solution)/shard_map/while/body/eval_jaxpr/all_to_all | solution.py:24
  576.7 7.8 %all-to-all-done = f32[16,1,8,2,128]{4,2,3,1,0:T(8,128)S(1)} async-done(((f32[16,1,8,2,128]{4,2,3,1,0:T(8,128)}), f32[16,1,8,2,128]{4,2,3,1,0:T(8,128)S(1)}, u32[]{:S(2)}, u32[]{:S(2)}) %all-to-all-start) | async-done | bytes 131104 | tf_op jit(solution)/shard_map/while/body/eval_jaxpr/all_to_all | solution.py:24
  (339 shorter events, 251.9 us)
Async XLA Ops:
  7.2 133.6 %all-gather.2.cloned.1.call-start = ((), (), s32[]{:S(2)}) async-start(), calls=%async_computation.6 | async-start | bytes 17825792 | tf_op jit(solution)/shard_map/all_gather | solution.py:76
  140.7 10.9 %copy-start = (bf16[1,2,2048,2048]{3,2,1,0:T(8,128)(2,1)S(1)}, bf16[1,2,2048,2048]{3,2,1,0:T(8,128)(2,1)}, u32[]{:S(2)}) copy-start(bf16[1,2,2048,2048]{3,2,1,0:T(8,128)(2,1)} %all-gather.2.cloned.1.call-done) | copy-start | bytes 50331652
  151.6 137.1 %copy-start.2 = (f32[128,2048,1]{1,0,2:T(8,128)}, f32[128,2048,1]{1,0,2:T(8,128)S(1)}, u32[]{:S(2)}) copy-start(f32[128,2048,1]{1,0,2:T(8,128)S(1)} %fusion.26) | copy-start | bytes 3145732
  247.9 5.8 copy-start.7
  249.0 19.7 %all-to-all-start.4 = ((f32[16,1,64,2,128]{4,2,3,1,0:T(8,128)}), f32[16,1,64,2,128]{4,2,3,1,0:T(8,128)S(1)}, u32[]{:S(2)}, u32[]{:S(2)}) async-start(f32[16,1,64,2,128]{4,2,3,1,0:T(8,128)} %broadcast_in_dim.75), calls=%async_computation.4 | async-start | bytes 2097152 | tf_op jit(solution)/shard_map/all_to_all | solution.py:24
  291.7 33.1 %all-to-all-start.5 = ((f32[16,1,64,2,128]{4,2,3,1,0:T(8,128)}), f32[16,1,64,2,128]{4,2,3,1,0:T(8,128)}, u32[]{:S(2)}, u32[]{:S(2)}) async-start(f32[16,1,64,2,128]{4,2,3,1,0:T(8,128)} %broadcast_in_dim.76), calls=%async_computation.5 | async-start | bytes 2097152 | tf_op jit(solution)/shard_map/all_to_all | solution.py:24
  347.1 11.5 %all-to-all-start = ((f32[16,1,8,2,128]{4,2,3,1,0:T(8,128)}), f32[16,1,8,2,128]{4,2,3,1,0:T(8,128)S(1)}, u32[]{:S(2)}, u32[]{:S(2)}) async-start(f32[16,1,8,2,128]{4,2,3,1,0:T(8,128)} %broadcast_in_dim.83), calls=%async_computation | async-start | bytes 262144 | tf_op jit(solution)/shard_map/while/body/eval_jaxpr/all_to_all | solution.py:24
  358.6 3.4 copy-start.3
  367.7 11.5 %all-to-all-start = ((f32[16,1,8,2,128]{4,2,3,1,0:T(8,128)}), f32[16,1,8,2,128]{4,2,3,1,0:T(8,128)S(1)}, u32[]{:S(2)}, u32[]{:S(2)}) async-start(f32[16,1,8,2,128]{4,2,3,1,0:T(8,128)} %broadcast_in_dim.83), calls=%async_computation | async-start | bytes 262144 | tf_op jit(solution)/shard_map/while/body/eval_jaxpr/all_to_all | solution.py:24
  379.1 3.4 copy-start.3
  388.2 11.5 %all-to-all-start = ((f32[16,1,8,2,128]{4,2,3,1,0:T(8,128)}), f32[16,1,8,2,128]{4,2,3,1,0:T(8,128)S(1)}, u32[]{:S(2)}, u32[]{:S(2)}) async-start(f32[16,1,8,2,128]{4,2,3,1,0:T(8,128)} %broadcast_in_dim.83), calls=%async_computation | async-start | bytes 262144 | tf_op jit(solution)/shard_map/while/body/eval_jaxpr/all_to_all | solution.py:24
  399.7 3.4 copy-start.3
  408.7 11.5 %all-to-all-start = ((f32[16,1,8,2,128]{4,2,3,1,0:T(8,128)}), f32[16,1,8,2,128]{4,2,3,1,0:T(8,128)S(1)}, u32[]{:S(2)}, u32[]{:S(2)}) async-start(f32[16,1,8,2,128]{4,2,3,1,0:T(8,128)} %broadcast_in_dim.83), calls=%async_computation | async-start | bytes 262144 | tf_op jit(solution)/shard_map/while/body/eval_jaxpr/all_to_all | solution.py:24
  420.2 3.4 copy-start.3
  429.3 11.5 %all-to-all-start = ((f32[16,1,8,2,128]{4,2,3,1,0:T(8,128)}), f32[16,1,8,2,128]{4,2,3,1,0:T(8,128)S(1)}, u32[]{:S(2)}, u32[]{:S(2)}) async-start(f32[16,1,8,2,128]{4,2,3,1,0:T(8,128)} %broadcast_in_dim.83), calls=%async_computation | async-start | bytes 262144 | tf_op jit(solution)/shard_map/while/body/eval_jaxpr/all_to_all | solution.py:24
  449.8 11.5 %all-to-all-start = ((f32[16,1,8,2,128]{4,2,3,1,0:T(8,128)}), f32[16,1,8,2,128]{4,2,3,1,0:T(8,128)S(1)}, u32[]{:S(2)}, u32[]{:S(2)}) async-start(f32[16,1,8,2,128]{4,2,3,1,0:T(8,128)} %broadcast_in_dim.83), calls=%async_computation | async-start | bytes 262144 | tf_op jit(solution)/shard_map/while/body/eval_jaxpr/all_to_all | solution.py:24
  461.3 3.4 copy-start.3
  470.4 11.5 %all-to-all-start = ((f32[16,1,8,2,128]{4,2,3,1,0:T(8,128)}), f32[16,1,8,2,128]{4,2,3,1,0:T(8,128)S(1)}, u32[]{:S(2)}, u32[]{:S(2)}) async-start(f32[16,1,8,2,128]{4,2,3,1,0:T(8,128)} %broadcast_in_dim.83), calls=%async_computation | async-start | bytes 262144 | tf_op jit(solution)/shard_map/while/body/eval_jaxpr/all_to_all | solution.py:24
  490.9 11.5 %all-to-all-start = ((f32[16,1,8,2,128]{4,2,3,1,0:T(8,128)}), f32[16,1,8,2,128]{4,2,3,1,0:T(8,128)S(1)}, u32[]{:S(2)}, u32[]{:S(2)}) async-start(f32[16,1,8,2,128]{4,2,3,1,0:T(8,128)} %broadcast_in_dim.83), calls=%async_computation | async-start | bytes 262144 | tf_op jit(solution)/shard_map/while/body/eval_jaxpr/all_to_all | solution.py:24
  511.4 11.5 %all-to-all-start = ((f32[16,1,8,2,128]{4,2,3,1,0:T(8,128)}), f32[16,1,8,2,128]{4,2,3,1,0:T(8,128)S(1)}, u32[]{:S(2)}, u32[]{:S(2)}) async-start(f32[16,1,8,2,128]{4,2,3,1,0:T(8,128)} %broadcast_in_dim.83), calls=%async_computation | async-start | bytes 262144 | tf_op jit(solution)/shard_map/while/body/eval_jaxpr/all_to_all | solution.py:24
  522.9 3.4 copy-start.3
  532.0 11.5 %all-to-all-start = ((f32[16,1,8,2,128]{4,2,3,1,0:T(8,128)}), f32[16,1,8,2,128]{4,2,3,1,0:T(8,128)S(1)}, u32[]{:S(2)}, u32[]{:S(2)}) async-start(f32[16,1,8,2,128]{4,2,3,1,0:T(8,128)} %broadcast_in_dim.83), calls=%async_computation | async-start | bytes 262144 | tf_op jit(solution)/shard_map/while/body/eval_jaxpr/all_to_all | solution.py:24
  552.5 11.5 %all-to-all-start = ((f32[16,1,8,2,128]{4,2,3,1,0:T(8,128)}), f32[16,1,8,2,128]{4,2,3,1,0:T(8,128)S(1)}, u32[]{:S(2)}, u32[]{:S(2)}) async-start(f32[16,1,8,2,128]{4,2,3,1,0:T(8,128)} %broadcast_in_dim.83), calls=%async_computation | async-start | bytes 262144 | tf_op jit(solution)/shard_map/while/body/eval_jaxpr/all_to_all | solution.py:24
  573.0 11.5 %all-to-all-start = ((f32[16,1,8,2,128]{4,2,3,1,0:T(8,128)}), f32[16,1,8,2,128]{4,2,3,1,0:T(8,128)S(1)}, u32[]{:S(2)}, u32[]{:S(2)}) async-start(f32[16,1,8,2,128]{4,2,3,1,0:T(8,128)} %broadcast_in_dim.83), calls=%async_computation | async-start | bytes 262144 | tf_op jit(solution)/shard_map/while/body/eval_jaxpr/all_to_all | solution.py:24
  (22 other events, 35.1 us)
Sparse Core Ops, SparseCore 0:
  28.9 111.8 all-gather.1
where the time goes:
time: 607 us; the launch traced here: 600 us
  waiting for transfers between devices  220 us (36%)
  matrix products  109 us (18%)
  blocking collectives  84.7 us (14%)
  other arithmetic  73.4 us (12%)
  starting transfers between devices  50.6 us (8%)
  local copies, waits for them, and re-layouts  45 us (7%)
  between operations  16 us (3%)
    all_gather x1, waiting for transfers between devices, shards(): gathered = lax.all_gather(turned, TILE, axis=2, tiled=True)  112 us
    all_to_all x14, waiting for transfers between devices, from_everyone(): lax.all_to_all(jnp.broadcast_to(shard[None], (devices, *shard.shape)), ax...  108 us
    all_to_all x14, starting transfers between devices, from_everyone(): lax.all_to_all(jnp.broadcast_to(shard[None], (devices, *shard.shape)), ax...  50.6 us
    all_to_all x2, blocking collectives, from_everyone(): lax.all_to_all(jnp.broadcast_to(shard[None], (devices, *shard.shape)), ax...  41.7 us
    dot_general x24, matrix products, project(): jnp.einsum('...bk,...kha->...bha', coefficients, subspace, precision=high...  35 us
    dot_general x15, matrix products, apply_rows(): jnp.einsum('...bhpa,...pra->...bhr', stacked, covariance, precision=highest)  26.4 us
    another operation x12, other arithmetic, orthonormal(): factor = jnp.linalg.cholesky(gram_matrix)  26.1 us
    psum x2, blocking collectives, one_axis_at_a_time(): return functools.reduce(lax.psum, axes, shard)  22.7 us
  transfers between devices with their start and end apart: 15, of which 14 were waited for; matrix products, arithmetic and copies ran while one was open for 1% of the time, Pallas kernels for 0%

commit v1 on v0

--- a/solution.py
+++ b/solution.py
@@ -73,7 +73,9 @@
     tile_total_count = lax.axis_size(TILE)
     block_row_set = ARRAY_ELEMENTS // tile_total_count
     first_row = lax.axis_index(TILE) * block_row_set
-    gathered = lax.all_gather(turned, TILE, axis=2, tiled=True)
+    gathered = jnp.concatenate(
+        lax.all_to_all(jnp.stack([turned] * lax.axis_size(TILE)), TILE, 0, 0), axis=2
+    )
     own_rows = lax.dynamic_slice_in_dim(gathered, first_row, block_row_set, 3)
     swapped = jnp.stack([own_rows[:, 1], -own_rows[:, 0]], 1)
     real_part = jnp.einsum("cpsi,cpsj->cij", own_rows, gathered, preferred_element_type=jnp.float32)

time: 607 us -> 812 us (1.34)
  waiting for transfers between devices: 220 us -> 356 us
  local copies, waits for them, and re-layouts: 45 us -> 113 us
  between operations: 16 us -> 2.76 us
  starting transfers between devices: 50.6 us -> 58.8 us
    all_to_all x0 -> x1, waiting for transfers between devices: none -> 248 us  [shards(): lax.all_to_all(jnp.stack([turned] * lax.axis_size(TILE)), TILE, 0, 0)]
    all_gather x1 -> x0, waiting for transfers between devices: 112 us -> none  [shards(): gathered = lax.all_gather(turned, TILE, axis=2, tiled=True)]
    reshape x0 -> x3, local copies, waits for them, and re-layouts: none -> 63.1 us  [shards(): jnp.concatenate(lax.all_to_all(jnp.stack([turned] * lax.axis_size(TILE)),...]
    all_to_all x0 -> x1, starting transfers between devices: none -> 8.23 us  [shards(): lax.all_to_all(jnp.stack([turned] * lax.axis_size(TILE)), TILE, 0, 0)]
where the time goes in v1:
time: 812 us; the launch traced here: 802 us
  waiting for transfers between devices  356 us (44%)
  matrix products  116 us (14%)
  local copies, waits for them, and re-layouts  113 us (14%)
  blocking collectives  81.6 us (10%)
  other arithmetic  73.7 us (9%)
  starting transfers between devices  58.8 us (7%)
    all_to_all x1, waiting for transfers between devices, shards(): lax.all_to_all(jnp.stack([turned] * lax.axis_size(TILE)), TILE, 0, 0)  248 us
    all_to_all x14, waiting for transfers between devices, from_everyone(): lax.all_to_all(jnp.broadcast_to(shard[None], (devices, *shard.shape)), ax...  108 us
    reshape x3, local copies, waits for them, and re-layouts, shards(): jnp.concatenate(lax.all_to_all(jnp.stack([turned] * lax.axis_size(TILE)),...  63.1 us
    all_to_all x14, starting transfers between devices, from_everyone(): lax.all_to_all(jnp.broadcast_to(shard[None], (devices, *shard.shape)), ax...  50.6 us
    all_to_all x2, blocking collectives, from_everyone(): lax.all_to_all(jnp.broadcast_to(shard[None], (devices, *shard.shape)), ax...  38.8 us
    dot_general x24, matrix products, project(): jnp.einsum('...bk,...kha->...bha', coefficients, subspace, precision=high...  35 us
    dot_general x15, matrix products, apply_rows(): jnp.einsum('...bhpa,...pra->...bhr', stacked, covariance, precision=highest)  26.4 us
    another operation x12, other arithmetic, orthonormal(): factor = jnp.linalg.cholesky(gram_matrix)  26.1 us
  transfers between devices with their start and end apart: 15, of which 14 were waited for; matrix products, arithmetic and copies ran while one was open for 1% of the time, Pallas kernels for 0%

profile of v1, /device:TPU:0, one launch (start us, length us, event | category | flops | bytes accessed | tf_op | source)
XLA Modules:
  0.0 802.4 jit_solution(17353037750736723979)
XLA Ops:
  2.3 20.2 %all_to_all.47 = bf16[8,2,128,256]{2,3,1,0:T(8,128)(2,1)S(1)} all-to-all(bf16[8,2,128,256]{2,3,1,0:T(8,128)(2,1)S(1)} %copy.84), channel_id=1, replica_groups=mesh['chan'=8,'tile_0'=4,'tile_1'=4] {'chan'}, dimensions={0} | all-to-all | bytes 2097152 | tf_op jit(solution)/shard_map/all_to_all | solution.py:72
  29.1 8.2 %all-to-all-start.2 = ((bf16[16,1,2,128,2048]{4,3,2,1,0:T(8,128)(2,1)}), bf16[16,1,2,128,2048]{4,3,2,1,0:T(8,128)(2,1)}, u32[]{:S(2)}, u32[]{:S(2)}) async-start(bf16[16,1,2,128,2048]{4,3,2,1,0:T(8,128)(2,1)} %stack.132), calls=%async_computation.2 | async-start | bytes 33554432 | tf_op jit(solution)/shard_map/all_to_all | solution.py:77
  37.4 247.9 %all-to-all-done.2 = bf16[16,1,2,128,2048]{4,3,2,1,0:T(8,128)(2,1)} async-done(((bf16[16,1,2,128,2048]{4,3,2,1,0:T(8,128)(2,1)}), bf16[16,1,2,128,2048]{4,3,2,1,0:T(8,128)(2,1)}, u32[]{:S(2)}, u32[]{:S(2)}) %all-to-all-start.2) | async-done | bytes 16777248 | tf_op jit(solution)/shard_map/all_to_all | solution.py:77
  285.3 14.1 %copy.88 = bf16[1,2,16,128,2048]{4,3,2,1,0:T(8,128)(2,1)} copy(bf16[1,2,16,128,2048]{4,3,1,0,2:T(8,128)(2,1)} %bitcast.3) | data formatting | bytes 33554432 | tf_op jit(solution)/shard_map/reshape | solution.py:76
  299.4 23.7 %copy.87 = bf16[1,2,16,128,2048]{3,2,4,1,0:T(8,128)(2,1)} copy(bf16[1,2,16,128,2048]{4,3,1,0,2:T(8,128)(2,1)} %bitcast.3) | data formatting | bytes 33554432 | tf_op jit(solution)/shard_map/reshape | solution.py:76
  323.1 25.3 %reshape.671 = bf16[1,2,2048,2048]{2,3,1,0:T(8,128)(2,1)} reshape(bf16[1,2,16,128,2048]{3,2,4,1,0:T(8,128)(2,1)} %copy.87) | data formatting | bytes 33554432 | tf_op jit(solution)/shard_map/reshape | solution.py:76
  349.8 8.4 %fusion.60 = f32[128,2048,1]{1,0,2:T(8,128)S(1)} fusion(bf16[2,2048,2048]{2,1,0:T(8,128)(2,1)} %bitcast.343, bf16[1,2,2048,2048]{2,3,1,0:T(8,128)(2,1)} %reshape.671, s32[]{:T(128)S(6)} %select_n.91), kind=kOutput, calls=%fused_computation.87 | convolution fusion | flops 2147483648 | bytes 18874372 | tf_op jit(solution)/shard_map/cpsi,cpsj->cij/dot_general | solution.py:81
  358.2 8.1 %fusion.41 = f32[128,2048,1]{1,0,2:T(8,128)S(1)} fusion(bf16[2,2048,2048]{2,1,0:T(8,128)(2,1)} %bitcast.344, bf16[1,1,2048,128]{2,3,1,0:T(8,128)(2,1)S(1)} %get-tuple-element.146, bf16[1,1,2048,128]{2,3,1,0:T(8,128)(2,1)S(1)} %get-tuple-element.145), kind=kOutput, calls=%fused_computation.62 | convolution fusion | flops 2148007936 | bytes 18874368 | tf_op jit(solution)/shard_map/cpsi,cpsj->cij/dot_general | solution.py:82
  374.6 20.6 %all_to_all.48 = f32[16,1,64,2,128]{4,2,3,1,0:T(8,128)S(1)} all-to-all(f32[16,1,64,2,128]{4,2,3,1,0:T(8,128)S(1)} %broadcast_in_dim.49), channel_id=1, replica_groups=mesh['chan'=8,'tile_0'=4,'tile_1'=4] {'tile_0','tile_1'}, dimensions={0} | all-to-all | bytes 2097152 | tf_op jit(solution)/shard_map/all_to_all | solution.py:24
  417.2 18.2 %all_to_all.49 = f32[16,1,64,2,128]{4,2,3,1,0:T(8,128)S(1)} all-to-all(f32[16,1,64,2,128]{4,2,3,1,0:T(8,128)S(1)} %broadcast_in_dim.74), channel_id=1, replica_groups=mesh['chan'=8,'tile_0'=4,'tile_1'=4] {'tile_0','tile_1'}, dimensions={0} | all-to-all | bytes 2097152 | tf_op jit(solution)/shard_map/all_to_all | solution.py:24
  462.9 14.0 %all-to-all-done.5 = f32[16,1,64,2,128]{4,2,3,1,0:T(8,128)S(1)} async-done(((f32[16,1,64,2,128]{4,2,3,1,0:T(8,128)}), f32[16,1,64,2,128]{4,2,3,1,0:T(8,128)S(1)}, u32[]{:S(2)}, u32[]{:S(2)}) %all-to-all-start.5) | async-done | bytes 1048608 | tf_op jit(solution)/shard_map/all_to_all | solution.py:24
  511.1 11.4 %psum.14 = f32[1]{0:T(128)} all-reduce(f32[1]{0:T(128)} %bitcast.93), channel_id=1, replica_groups=mesh['chan'=8,'tile_0'=4,'tile_1'=4] {'tile_0'}, use_global_device_ids=true, to_apply=%region_4.7 | all-reduce | flops 1 | bytes 8 | tf_op jit(solution)/shard_map/psum | solution.py:19
  522.5 11.3 %psum.15 = f32[1]{0:T(128)} all-reduce(f32[1]{0:T(128)} %psum.14), channel_id=1, replica_groups=mesh['chan'=8,'tile_0'=4,'tile_1'=4] {'tile_1'}, use_global_device_ids=true, to_apply=%region_5.8 | all-reduce | flops 1 | bytes 8 | tf_op jit(solution)/shard_map/psum | solution.py:19
  552.8 246.5 %while.17 = (s32[]{:T(128)}, f32[1,8,2,2048]{3,1,2,0:T(8,128)}, f32[1,8,2,2048]{3,1,2,0:T(8,128)}, f32[1,8,2,2048]{3,1,2,0:T(8,128)S(1)}, f32[1,8]{1,0:T(1,128)S...) while((s32[]{:T(128)}, f32[1,8,2,2048]{3,1,2,0:T(8,128)}, ...), condition=%wide.region_10.13_spmd.clone, body=%wide.region_6.12_spmd.clone.sunk | while | flops 202031136 | bytes 11035327 | solution.py:127
  560.5 7.8 all-to-all-done
  581.0 7.8 all-to-all-done
  601.5 7.8 all-to-all-done
  622.1 7.8 all-to-all-done
  642.6 7.8 all-to-all-done
  663.2 7.8 all-to-all-done
  683.7 7.8 all-to-all-done
  704.2 7.8 all-to-all-done
  745.3 7.8 all-to-all-done
  765.9 7.8 all-to-all-done
  (344 shorter events, 289.2 us)
Async XLA Ops:
  29.1 8.2 %copy-start.8 = (s32[1,32]{1,0:T(1,128)S(1)}, s32[1,32]{1,0:T(1,128)}, u32[]{:S(2)}) copy-start(s32[1,32]{1,0:T(1,128)} %param.12) | copy-start | bytes 388
  29.1 256.2 %all-to-all-start.2 = ((bf16[16,1,2,128,2048]{4,3,2,1,0:T(8,128)(2,1)}), bf16[16,1,2,128,2048]{4,3,2,1,0:T(8,128)(2,1)}, u32[]{:S(2)}, u32[]{:S(2)}) async-start(bf16[16,1,2,128,2048]{4,3,2,1,0:T(8,128)(2,1)} %stack.132), calls=%async_computation.2 | async-start | bytes 33554432 | tf_op jit(solution)/shard_map/all_to_all | solution.py:77
  366.4 132.7 %copy-start.1 = (f32[128,2048,1]{1,0,2:T(8,128)}, f32[128,2048,1]{1,0,2:T(8,128)S(1)}, u32[]{:S(2)}) copy-start(f32[128,2048,1]{1,0,2:T(8,128)S(1)} %fusion.41) | copy-start | bytes 3145732
  457.3 5.2 copy-start.7
  458.4 18.5 %all-to-all-start.5 = ((f32[16,1,64,2,128]{4,2,3,1,0:T(8,128)}), f32[16,1,64,2,128]{4,2,3,1,0:T(8,128)S(1)}, u32[]{:S(2)}, u32[]{:S(2)}) async-start(f32[16,1,64,2,128]{4,2,3,1,0:T(8,128)} %broadcast_in_dim.75), calls=%async_computation.5 | async-start | bytes 2097152 | tf_op jit(solution)/shard_map/all_to_all | solution.py:24
  462.8 43.6 %copy-start.5 = (f32[1,8,1,2048]{3,1,2,0:T(8,128)}, f32[1,8,1,2048]{3,1,2,0:T(8,128)S(1)}, u32[]{:S(2)}) copy-start(f32[1,8,1,2048]{3,1,2,0:T(8,128)S(1)} %get-tuple-element.169) | copy-start | bytes 196612
  462.9 43.6 %copy-start.6 = (f32[1,8,1,2048]{3,1,2,0:T(8,128)}, f32[1,8,1,2048]{3,1,2,0:T(8,128)S(1)}, u32[]{:S(2)}) copy-start(f32[1,8,1,2048]{3,1,2,0:T(8,128)S(1)} %get-tuple-element.170) | copy-start | bytes 196612
  502.1 32.3 %all-to-all-start.6 = ((f32[16,1,64,2,128]{4,2,3,1,0:T(8,128)}), f32[16,1,64,2,128]{4,2,3,1,0:T(8,128)}, u32[]{:S(2)}, u32[]{:S(2)}) async-start(f32[16,1,64,2,128]{4,2,3,1,0:T(8,128)} %broadcast_in_dim.76), calls=%async_computation.6 | async-start | bytes 2097152 | tf_op jit(solution)/shard_map/all_to_all | solution.py:24
  556.8 11.5 %all-to-all-start = ((f32[16,1,8,2,128]{4,2,3,1,0:T(8,128)}), f32[16,1,8,2,128]{4,2,3,1,0:T(8,128)S(1)}, u32[]{:S(2)}, u32[]{:S(2)}) async-start(f32[16,1,8,2,128]{4,2,3,1,0:T(8,128)} %broadcast_in_dim.83), calls=%async_computation | async-start | bytes 262144 | tf_op jit(solution)/shard_map/while/body/eval_jaxpr/all_to_all | solution.py:24
  568.3 3.4 copy-start.3
  577.3 11.5 %all-to-all-start = ((f32[16,1,8,2,128]{4,2,3,1,0:T(8,128)}), f32[16,1,8,2,128]{4,2,3,1,0:T(8,128)S(1)}, u32[]{:S(2)}, u32[]{:S(2)}) async-start(f32[16,1,8,2,128]{4,2,3,1,0:T(8,128)} %broadcast_in_dim.83), calls=%async_computation | async-start | bytes 262144 | tf_op jit(solution)/shard_map/while/body/eval_jaxpr/all_to_all | solution.py:24
  588.8 3.4 copy-start.3
  597.9 11.5 %all-to-all-start = ((f32[16,1,8,2,128]{4,2,3,1,0:T(8,128)}), f32[16,1,8,2,128]{4,2,3,1,0:T(8,128)S(1)}, u32[]{:S(2)}, u32[]{:S(2)}) async-start(f32[16,1,8,2,128]{4,2,3,1,0:T(8,128)} %broadcast_in_dim.83), calls=%async_computation | async-start | bytes 262144 | tf_op jit(solution)/shard_map/while/body/eval_jaxpr/all_to_all | solution.py:24
  609.3 3.4 copy-start.3
  618.4 11.5 %all-to-all-start = ((f32[16,1,8,2,128]{4,2,3,1,0:T(8,128)}), f32[16,1,8,2,128]{4,2,3,1,0:T(8,128)S(1)}, u32[]{:S(2)}, u32[]{:S(2)}) async-start(f32[16,1,8,2,128]{4,2,3,1,0:T(8,128)} %broadcast_in_dim.83), calls=%async_computation | async-start | bytes 262144 | tf_op jit(solution)/shard_map/while/body/eval_jaxpr/all_to_all | solution.py:24
  639.0 11.5 %all-to-all-start = ((f32[16,1,8,2,128]{4,2,3,1,0:T(8,128)}), f32[16,1,8,2,128]{4,2,3,1,0:T(8,128)S(1)}, u32[]{:S(2)}, u32[]{:S(2)}) async-start(f32[16,1,8,2,128]{4,2,3,1,0:T(8,128)} %broadcast_in_dim.83), calls=%async_computation | async-start | bytes 262144 | tf_op jit(solution)/shard_map/while/body/eval_jaxpr/all_to_all | solution.py:24
  659.5 11.5 %all-to-all-start = ((f32[16,1,8,2,128]{4,2,3,1,0:T(8,128)}), f32[16,1,8,2,128]{4,2,3,1,0:T(8,128)S(1)}, u32[]{:S(2)}, u32[]{:S(2)}) async-start(f32[16,1,8,2,128]{4,2,3,1,0:T(8,128)} %broadcast_in_dim.83), calls=%async_computation | async-start | bytes 262144 | tf_op jit(solution)/shard_map/while/body/eval_jaxpr/all_to_all | solution.py:24
  680.0 11.5 %all-to-all-start = ((f32[16,1,8,2,128]{4,2,3,1,0:T(8,128)}), f32[16,1,8,2,128]{4,2,3,1,0:T(8,128)S(1)}, u32[]{:S(2)}, u32[]{:S(2)}) async-start(f32[16,1,8,2,128]{4,2,3,1,0:T(8,128)} %broadcast_in_dim.83), calls=%async_computation | async-start | bytes 262144 | tf_op jit(solution)/shard_map/while/body/eval_jaxpr/all_to_all | solution.py:24
  700.6 11.5 %all-to-all-start = ((f32[16,1,8,2,128]{4,2,3,1,0:T(8,128)}), f32[16,1,8,2,128]{4,2,3,1,0:T(8,128)S(1)}, u32[]{:S(2)}, u32[]{:S(2)}) async-start(f32[16,1,8,2,128]{4,2,3,1,0:T(8,128)} %broadcast_in_dim.83), calls=%async_computation | async-start | bytes 262144 | tf_op jit(solution)/shard_map/while/body/eval_jaxpr/all_to_all | solution.py:24
  721.1 11.5 %all-to-all-start = ((f32[16,1,8,2,128]{4,2,3,1,0:T(8,128)}), f32[16,1,8,2,128]{4,2,3,1,0:T(8,128)S(1)}, u32[]{:S(2)}, u32[]{:S(2)}) async-start(f32[16,1,8,2,128]{4,2,3,1,0:T(8,128)} %broadcast_in_dim.83), calls=%async_computation | async-start | bytes 262144 | tf_op jit(solution)/shard_map/while/body/eval_jaxpr/all_to_all | solution.py:24
  741.6 11.5 %all-to-all-start = ((f32[16,1,8,2,128]{4,2,3,1,0:T(8,128)}), f32[16,1,8,2,128]{4,2,3,1,0:T(8,128)S(1)}, u32[]{:S(2)}, u32[]{:S(2)}) async-start(f32[16,1,8,2,128]{4,2,3,1,0:T(8,128)} %broadcast_in_dim.83), calls=%async_computation | async-start | bytes 262144 | tf_op jit(solution)/shard_map/while/body/eval_jaxpr/all_to_all | solution.py:24
  753.1 3.4 copy-start.3
  762.2 11.5 %all-to-all-start = ((f32[16,1,8,2,128]{4,2,3,1,0:T(8,128)}), f32[16,1,8,2,128]{4,2,3,1,0:T(8,128)S(1)}, u32[]{:S(2)}, u32[]{:S(2)}) async-start(f32[16,1,8,2,128]{4,2,3,1,0:T(8,128)} %broadcast_in_dim.83), calls=%async_computation | async-start | bytes 262144 | tf_op jit(solution)/shard_map/while/body/eval_jaxpr/all_to_all | solution.py:24
  782.7 11.5 %all-to-all-start = ((f32[16,1,8,2,128]{4,2,3,1,0:T(8,128)}), f32[16,1,8,2,128]{4,2,3,1,0:T(8,128)S(1)}, u32[]{:S(2)}, u32[]{:S(2)}) async-start(f32[16,1,8,2,128]{4,2,3,1,0:T(8,128)} %broadcast_in_dim.83), calls=%async_computation | async-start | bytes 262144 | tf_op jit(solution)/shard_map/while/body/eval_jaxpr/all_to_all | solution.py:24
  (22 other events, 39.0 us)
